TPU v7x, 8 devices: a whole 2x2x1 slice. The times are simulated.
8 devices in a mesh: data: 2 (over z, y), seq: 4 (over x, core).
Axes of the slice: x: 2, y: 2, z: 1, core: 2. Of those that a mesh axis runs over, the one named last changes fastest.
Arguments:
- x_in: bfloat16 [4096, 4096], P(('data', 'seq')), parts along dimension 0
- g_attn: float32 [4096], replicated
- w_qkv: bfloat16 [4096, 12288], replicated
- w_out: bfloat16 [16, 256, 4096], replicated
- g_mlp: float32 [4096], replicated
- w_gate: bfloat16 [4096, 16384], replicated
- w_up: bfloat16 [4096, 16384], replicated
- w_down: bfloat16 [16384, 4096], replicated
Outputs:
- output: bfloat16 [4096, 4096], P(('data', 'seq')), parts along dimension 0
There are 2 independent parts. A program takes and returns all parts, laid end to end along the dimension named above; an argument that names none is the same for every part.
All inputs are finite; a program needn't handle non-finite values.
Results may differ from a plain program's by a relative error of at most 0.00758202.
Values are sent between devices in bfloat16 or wider.
A program may use at most 2.25 GiB of HBM per device.

v0:
```python
import jax
import jax.numpy as jnp
from jax import lax
from jax.sharding import PartitionSpec as P

ROPE_BASE = 10000


def rms_norm(row_vals, gain_vec):
    rows_f32 = row_vals.astype(jnp.float32)
    inv_rms = lax.rsqrt(jnp.mean(rows_f32 * rows_f32, axis=-1, keepdims=True) + 1e-5)
    return (rows_f32 * inv_rms * gain_vec).astype(jnp.bfloat16)


def rope_tables(positions, head_dim):
    inv_freq = 1.0 / (ROPE_BASE ** (jnp.arange(0, head_dim, 2, dtype=jnp.float32) / head_dim))
    angles = positions.astype(jnp.float32)[:, None] * inv_freq[None, :]
    angles = jnp.concatenate([angles, angles], axis=-1)
    return jnp.cos(angles), jnp.sin(angles)


def apply_rope(qk_pair, cos_tab, sin_tab):
    half_dim = qk_pair.shape[-1] // 2
    rotated = jnp.concatenate([-qk_pair[..., half_dim:], qk_pair[..., :half_dim]], axis=-1)
    return qk_pair * cos_tab + rotated * sin_tab


def gated_mlp(y_rows, g_mlp, w_gate, w_up, w_down):
    y_norm = rms_norm(y_rows, g_mlp)
    gate_pre = jnp.dot(y_norm, w_gate, preferred_element_type=jnp.float32)
    up_pre = jnp.dot(y_norm, w_up, preferred_element_type=jnp.float32)
    hidden = (jax.nn.silu(gate_pre) * up_pre).astype(jnp.bfloat16)
    return (y_rows.astype(jnp.float32) + jnp.dot(hidden, w_down, preferred_element_type=jnp.float32)).astype(jnp.bfloat16)


def causal_attention(packed, block_rows):
    total_rows = packed.shape[0]
    local_heads = packed.shape[2]
    head_dim = packed.shape[3]
    query_rows = packed[:, 0]
    key_rows = packed[:, 1]
    value_rows = packed[:, 2]
    score_scale = head_dim ** -0.5
    key_pos = jnp.arange(total_rows)

    def one_block(block_idx):
        row_start = block_idx * block_rows
        q_blk = lax.dynamic_slice_in_dim(query_rows, row_start, block_rows, axis=0)
        scores = jnp.einsum('qhd,khd->hqk', q_blk, key_rows, preferred_element_type=jnp.float32) * score_scale
        query_pos = row_start + jnp.arange(block_rows)
        allowed = key_pos[None, :] <= query_pos[:, None]
        scores = jnp.where(allowed[None], scores, -jnp.inf)
        attn_probs = jax.nn.softmax(scores, axis=-1).astype(jnp.bfloat16)
        return jnp.einsum('hqk,khd->qhd', attn_probs, value_rows, preferred_element_type=jnp.float32).astype(jnp.bfloat16)

    blocks = lax.map(one_block, jnp.arange(total_rows // block_rows))
    return blocks.reshape(total_rows, local_heads, head_dim)


def solution(mesh):
    def local_layer(x_blk, g_attn, w_qkv, w_out, g_mlp, w_gate, w_up, w_down):
        n_heads, head_dim, model_width = w_out.shape
        local_rows = x_blk.shape[0]
        member = lax.axis_index('seq')
        x_norm = rms_norm(x_blk, g_attn)
        qkv_f32 = jnp.dot(x_norm, w_qkv, preferred_element_type=jnp.float32).reshape(local_rows, 3, n_heads, head_dim)
        positions = member * local_rows + jnp.arange(local_rows)
        cos_tab, sin_tab = rope_tables(positions, head_dim)
        qk_rot = apply_rope(qkv_f32[:, :2], cos_tab[:, None, None, :], sin_tab[:, None, None, :])
        packed = jnp.concatenate([qk_rot, qkv_f32[:, 2:]], axis=1).astype(jnp.bfloat16)
        head_major = lax.all_to_all(packed, 'seq', 2, 0, tiled=True)
        attn_heads = causal_attention(head_major, local_rows)
        attn_rows = lax.all_to_all(attn_heads, 'seq', 0, 1, tiled=True)
        attn_mixed = jnp.dot(attn_rows.reshape(local_rows, n_heads * head_dim), w_out.reshape(n_heads * head_dim, model_width), preferred_element_type=jnp.float32)
        y_rows = (x_blk.astype(jnp.float32) + attn_mixed).astype(jnp.bfloat16)
        return gated_mlp(y_rows, g_mlp, w_gate, w_up, w_down)

    row_spec = P(('data', 'seq'), None)
    return jax.shard_map(local_layer, mesh=mesh, in_specs=(row_spec, P(), P(), P(), P(), P(), P(), P()), out_specs=row_spec, check_vma=False)
```

profile of v0, /device:TPU:0, one launch (start us, length us, event | category | flops | bytes accessed | tf_op | source)
XLA Modules:
  0.0 746.2 jit_solution(10558907807160887956)
XLA Ops:
  0.0 3.1 fusion.30
  3.1 61.2 %fusion.38 = f32[512,12288]{1,0:T(8,128)} fusion(bf16[4096,12288]{1,0:T(8,128)(2,1)} %param.12, bf16[512,4096]{1,0:T(8,128)(2,1)} %param.10, f32[4096]{0:T(1024)} %param.11, f32[512]{0:T(512)S(1)} %add_rsqrt_fusion.1), kind=kOutput, calls=%fused_computation.47 | convolution fusion | flops 51547996160 | bytes 130041856 | tf_op jit(solution)/shard_map/dot_general | solution.py:66
  64.3 23.2 %copy.44 = f32[64,8,48,256]{3,2,1,0:T(8,128)} copy(f32[64,8,48,256]{3,1,2,0:T(8,128)} %bitcast.56) | data formatting | bytes 50331648
  87.4 4.0 slice.34
  91.4 12.3 %slice.31 = f32[512,2,16,256]{3,2,1,0:T(8,128)} slice(f32[512,3,16,256]{3,2,1,0:T(8,128)} %bitcast.53), slice={[0:512], [0:2], [0:16], [0:256]} | slice | bytes 33554432 | tf_op jit(solution)/shard_map/slice | solution.py:69
  103.7 7.1 fusion.57
  110.8 3.6 copy.52
  114.5 8.1 %copy.42 = f32[512,2,16,128]{3,0,1,2:T(8,128)} copy(f32[512,2,16,128]{3,2,1,0:T(8,128)S(1)} %get-tuple-element.72) | data formatting | bytes 16777216
  122.5 8.8 %copy_negate_fusion = f32[512,2,16,128]{3,0,1,2:T(8,128)} fusion(f32[512,2,16,128]{3,2,1,0:T(8,128)S(1)} %get-tuple-element.71), kind=kLoop, calls=%fused_computation.46 | loop fusion | flops 2097152 | bytes 16777216 | tf_op jit(solution)/shard_map/neg | solution.py:24
  131.3 0.1 broadcast_multiply_fusion
  131.5 1.9 fusion.50
  133.4 0.0 copy-start
  133.4 17.6 %fusion.28 = bf16[512,2,16,256]{3,0,1,2:T(8,128)(2,1)S(1)} fusion(f32[512,2,16,256]{3,2,1,0:T(8,128)} %slice.31, f32[512,2,16,128]{3,0,1,2:T(8,128)} %copy.42, f32[512,2,16,128]{3,0,1,2:T(8,128)} %copy_negate_fusion, f32[512,256]{1,0:T(8,128)S(1)} %get-tuple-element.77, f32[512,256]{1,0:T(8,128)S(1)} %get-tuple-element.76), kind=kLoop, calls=%fused_computation.27 | loop fusion | flops 20971520 | bytes 42991616 | tf_op jit(solution)/shard_map/convert
  151.0 0.0 copy-done
  151.0 7.0 pad_maximum_fusion
  158.0 6.6 all-to-all-start
  164.6 138.8 %all-to-all-done = bf16[512,3,16,256]{3,0,1,2:T(8,128)(2,1)} async-done(((bf16[512,3,16,256]{3,0,1,2:T(8,128)(2,1)}), bf16[512,3,16,256]{3,0,1,2:T(8,128)(2,1)}, u32[]{:S(2)}, u32[]{:S(2)}) %all-to-all-start) | async-done | bytes 12582944 | tf_op jit(solution)/shard_map/all_to_all | solution.py:71
  303.4 6.1 copy.33
  309.5 4.6 slice_bitcast_fusion
  314.1 93.2 %while.11 = (s32[]{:T(128)}, bf16[4,512,4,256]{3,1,0,2:T(8,128)(2,1)}, s32[4]{0:T(128)S(1)}, bf16[2048,4,256]{2,0,1:T(8,128)(2,1)}, bf16[2048,4,256]{2,0,1:T(8,1...) while((s32[]{:T(128)}, ...), condition=%wide.region_4.5_spmd.clone, body=%wide.region_1.4_spmd.clone.sunk | while | flops 4321708544 | bytes 46158000 | solution.py:56
  314.1 0.7 dynamic_slice.24
  315.5 0.7 iota_compare_fusion.2
  316.2 11.0 %fusion.89 = (f32[4,512]{1,0:T(4,128)S(1)}, f32[4,512,2048]{2,1,0:T(8,128)}) fusion(pred[512,2048]{1,0:T(8,128)(4,1)S(1)} %iota_compare_fusion.2, bf16[2048,4,256]{2,0,1:T(8,128)(2,1)} %get-tuple-element.145, bf16[2048,4,256]{2,0,1:T(8,128)(2,1)} %get-tuple-element.144, s32[]{:T(128)S(6)} %select_n.22), kind=kOutput, calls=%fused_computation.65.clone.1 | convolution fusion | flops 2164262912 | bytes 23076868 | tf_op jit(solution)/shard_map/while/body/eval_jaxpr/sub | solution.py:53
  327.1 10.3 %fusion.90 = bf16[4,512,4,256]{3,1,0,2:T(8,128)(2,1)} fusion(bf16[4,512,4,256]{3,1,0,2:T(8,128)(2,1)} %get-tuple-element.132, s32[]{:T(128)S(6)} %copy.56, bf16[2048,4,256]{2,0,1:T(8,128)(2,1)} %get-tuple-element.146, f32[4,512,2048]{2,1,0:T(8,128)} %get-tuple-element.119, f32[4,512]{1,0:T(4,128)S(1)} %get-tuple-element.120), kind=kOutput, calls=%fused_computation.13.clone.1 | convolution fusion | flops 2156396544 | bytes 22028292 | tf_op jit(solution)/shard_map/while/body/eval_jaxpr/hqk,khd->qhd/dot_general | solution.py:54
  337.4 0.7 dynamic_slice.24
  338.8 0.7 iota_compare_fusion.2
  339.5 11.0 %fusion.89 = (f32[4,512]{1,0:T(4,128)S(1)}, f32[4,512,2048]{2,1,0:T(8,128)}) fusion(pred[512,2048]{1,0:T(8,128)(4,1)S(1)} %iota_compare_fusion.2, bf16[2048,4,256]{2,0,1:T(8,128)(2,1)} %get-tuple-element.145, bf16[2048,4,256]{2,0,1:T(8,128)(2,1)} %get-tuple-element.144, s32[]{:T(128)S(6)} %select_n.22), kind=kOutput, calls=%fused_computation.65.clone.1 | convolution fusion | flops 2164262912 | bytes 23076868 | tf_op jit(solution)/shard_map/while/body/eval_jaxpr/sub | solution.py:53
  350.4 10.3 %fusion.90 = bf16[4,512,4,256]{3,1,0,2:T(8,128)(2,1)} fusion(bf16[4,512,4,256]{3,1,0,2:T(8,128)(2,1)} %get-tuple-element.132, s32[]{:T(128)S(6)} %copy.56, bf16[2048,4,256]{2,0,1:T(8,128)(2,1)} %get-tuple-element.146, f32[4,512,2048]{2,1,0:T(8,128)} %get-tuple-element.119, f32[4,512]{1,0:T(4,128)S(1)} %get-tuple-element.120), kind=kOutput, calls=%fused_computation.13.clone.1 | convolution fusion | flops 2156396544 | bytes 22028292 | tf_op jit(solution)/shard_map/while/body/eval_jaxpr/hqk,khd->qhd/dot_general | solution.py:54
  360.7 0.7 dynamic_slice.24
  362.1 0.7 iota_compare_fusion.2
  362.8 11.0 %fusion.89 = (f32[4,512]{1,0:T(4,128)S(1)}, f32[4,512,2048]{2,1,0:T(8,128)}) fusion(pred[512,2048]{1,0:T(8,128)(4,1)S(1)} %iota_compare_fusion.2, bf16[2048,4,256]{2,0,1:T(8,128)(2,1)} %get-tuple-element.145, bf16[2048,4,256]{2,0,1:T(8,128)(2,1)} %get-tuple-element.144, s32[]{:T(128)S(6)} %select_n.22), kind=kOutput, calls=%fused_computation.65.clone.1 | convolution fusion | flops 2164262912 | bytes 23076868 | tf_op jit(solution)/shard_map/while/body/eval_jaxpr/sub | solution.py:53
  373.7 10.3 %fusion.90 = bf16[4,512,4,256]{3,1,0,2:T(8,128)(2,1)} fusion(bf16[4,512,4,256]{3,1,0,2:T(8,128)(2,1)} %get-tuple-element.132, s32[]{:T(128)S(6)} %copy.56, bf16[2048,4,256]{2,0,1:T(8,128)(2,1)} %get-tuple-element.146, f32[4,512,2048]{2,1,0:T(8,128)} %get-tuple-element.119, f32[4,512]{1,0:T(4,128)S(1)} %get-tuple-element.120), kind=kOutput, calls=%fused_computation.13.clone.1 | convolution fusion | flops 2156396544 | bytes 22028292 | tf_op jit(solution)/shard_map/while/body/eval_jaxpr/hqk,khd->qhd/dot_general | solution.py:54
  384.1 0.7 dynamic_slice.24
  385.4 0.7 iota_compare_fusion.2
  386.1 11.0 %fusion.89 = (f32[4,512]{1,0:T(4,128)S(1)}, f32[4,512,2048]{2,1,0:T(8,128)}) fusion(pred[512,2048]{1,0:T(8,128)(4,1)S(1)} %iota_compare_fusion.2, bf16[2048,4,256]{2,0,1:T(8,128)(2,1)} %get-tuple-element.145, bf16[2048,4,256]{2,0,1:T(8,128)(2,1)} %get-tuple-element.144, s32[]{:T(128)S(6)} %select_n.22), kind=kOutput, calls=%fused_computation.65.clone.1 | convolution fusion | flops 2164262912 | bytes 23076868 | tf_op jit(solution)/shard_map/while/body/eval_jaxpr/sub | solution.py:53
  397.1 10.3 %fusion.90 = bf16[4,512,4,256]{3,1,0,2:T(8,128)(2,1)} fusion(bf16[4,512,4,256]{3,1,0,2:T(8,128)(2,1)} %get-tuple-element.132, s32[]{:T(128)S(6)} %copy.56, bf16[2048,4,256]{2,0,1:T(8,128)(2,1)} %get-tuple-element.146, f32[4,512,2048]{2,1,0:T(8,128)} %get-tuple-element.119, f32[4,512]{1,0:T(4,128)S(1)} %get-tuple-element.120), kind=kOutput, calls=%fused_computation.13.clone.1 | convolution fusion | flops 2156396544 | bytes 22028292 | tf_op jit(solution)/shard_map/while/body/eval_jaxpr/hqk,khd->qhd/dot_general | solution.py:54
  407.4 5.8 copy.35
  413.1 51.2 %all_to_all.33 = bf16[2048,4,256]{2,1,0:T(4,128)(2,1)S(1)} all-to-all(bf16[2048,4,256]{2,1,0:T(4,128)(2,1)S(1)} %copy.35), channel_id=1, replica_groups=mesh['data'=2,'seq'=4] {'seq'}, dimensions={0} | all-to-all | bytes 8388608 | tf_op jit(solution)/shard_map/all_to_all | solution.py:73
  464.3 2.6 copy.36
  466.9 7.3 copy.37
  474.2 0.0 copy-start.1
  474.2 27.6 %fusion.34 = (f32[512]{0:T(512)S(1)}, bf16[512,4096]{1,0:T(8,128)(2,1)}) fusion(bf16[512,4096]{0,1:T(8,128)(2,1)} %bitcast.59, bf16[4096,4096]{1,0:T(8,128)(2,1)} %bitcast.60, bf16[512,4096]{1,0:T(8,128)(2,1)} %param.10), kind=kOutput, calls=%fused_computation.41 | convolution fusion | flops 17192452096 | bytes 46139392 | tf_op jit(solution)/shard_map/dot_general | solution.py:74
  501.8 0.0 copy-done.1
  501.8 80.0 %fusion.42 = f32[512,16384]{1,0:T(8,128)} fusion(bf16[4096,16384]{1,0:T(8,128)(2,1)} %param.15, bf16[512,4096]{1,0:T(8,128)(2,1)} %get-tuple-element.79, f32[4096]{0:T(1024)S(1)} %copy-done.1, f32[512]{0:T(512)S(1)} %add_rsqrt_fusion), kind=kOutput, calls=%fused_computation.51 | convolution fusion | flops 68727865344 | bytes 171984896 | tf_op jit(solution)/shard_map/dot_general | solution.py:30
  581.9 81.9 %multiply_convert_fusion.clone.6 = bf16[512,16384]{1,0:T(8,128)(2,1)} fusion(f32[512,16384]{1,0:T(8,128)} %fusion.42, bf16[4096,16384]{1,0:T(8,128)(2,1)} %param.16, bf16[512,4096]{1,0:T(8,128)(2,1)} %get-tuple-element.79, f32[4096]{0:T(1024)S(1)} %copy-done.1, f32[512]{0:T(512)S(1)} %add_rsqrt_fusion), kind=kOutput, calls=%fused_computation.23.clone.clone.clone.clone.clone.1 | convolution fusion | flops 68778196992 | bytes 188762112 | tf_op jit(solution)/shard_map/dot_general | solution.py:31
  663.8 82.2 %fusion.37 = bf16[512,4096]{1,0:T(8,128)(2,1)} fusion(bf16[512,4096]{1,0:T(8,128)(2,1)} %get-tuple-element.79, bf16[16384,4096]{1,0:T(8,128)(2,1)} %param.17, bf16[512,16384]{1,0:T(8,128)(2,1)} %multiply_convert_fusion.clone.6), kind=kOutput, calls=%fused_computation.44 | convolution fusion | flops 68725768192 | bytes 159383552 | tf_op jit(solution)/shard_map/dot_general | solution.py:33
  (10 shorter events, 0.1 us)
Async XLA Ops:
  133.4 17.6 %copy-start = (bf16[512,1,16,256]{3,0,1,2:T(8,128)(2,1)S(1)}, bf16[512,1,16,256]{3,0,1,2:T(8,128)(2,1)}, u32[]{:S(2)}) copy-start(bf16[512,1,16,256]{3,0,1,2:T(8,128)(2,1)} %copy.52) | copy-start | bytes 12582916
  158.0 145.4 %all-to-all-start = ((bf16[512,3,16,256]{3,0,1,2:T(8,128)(2,1)}), bf16[512,3,16,256]{3,0,1,2:T(8,128)(2,1)}, u32[]{:S(2)}, u32[]{:S(2)}) async-start(bf16[512,3,16,256]{3,0,1,2:T(8,128)(2,1)} %pad_maximum_fusion), calls=%async_computation | async-start | bytes 25165824 | tf_op jit(solution)/shard_map/all_to_all | solution.py:71
  474.2 27.7 %copy-start.1 = (f32[4096]{0:T(1024)S(1)}, f32[4096]{0:T(1024)}, u32[]{:S(2)}) copy-start(f32[4096]{0:T(1024)} %param.14) | copy-start | bytes 49156
where the time goes:
time: 754 us; the launch traced here: 746 us
  matrix products  418 us (55%)
  waiting for transfers between devices  139 us (18%)
  local copies, waits for them, and re-layouts  87.3 us (12%)
  blocking collectives  51.2 us (7%)
  other arithmetic  41.2 us (5%)
    all_to_all x1, waiting for transfers between devices, local_layer(): head_major = lax.all_to_all(packed, 'seq', 2, 0, tiled=True)  139 us
    dot_general x1, matrix products, gated_mlp(): jnp.dot(hidden, w_down, preferred_element_type=jnp.float32)  82.2 us
    dot_general x1, matrix products, gated_mlp(): up_pre = jnp.dot(y_norm, w_up, preferred_element_type=jnp.float32)  81.9 us
    dot_general x1, matrix products, gated_mlp(): gate_pre = jnp.dot(y_norm, w_gate, preferred_element_type=jnp.float32)  80 us
    dot_general x1, matrix products, local_layer(): jnp.dot(x_norm, w_qkv, preferred_element_type=jnp.float32)  61.2 us
    all_to_all x1, blocking collectives, local_layer(): attn_rows = lax.all_to_all(attn_heads, 'seq', 0, 1, tiled=True)  51.2 us
    sub x4, matrix products, one_block(): attn_probs = jax.nn.softmax(scores, axis=-1).astype(jnp.bfloat16)  43.9 us
    dot_general x4, matrix products, one_block(): jnp.einsum('hqk,khd->qhd', attn_probs, value_rows, preferred_element_type...  41.2 us
  transfers between devices with their start and end apart: 1, of which 1 were waited for; matrix products, arithmetic and copies ran while one was open for 0% of the time, Pallas kernels for 0%

commit v1 on v0

v1 whole, which is shorter than its diff:
```python
import functools

import jax
import jax.numpy as jnp
from jax import lax
from jax.experimental import pallas as pl
from jax.experimental.pallas import tpu as pltpu
from jax.sharding import PartitionSpec as P

ROPE_BASE = 10000
F32 = jnp.float32
BF16 = jnp.bfloat16
LOG2E = 1.4426950408889634
VMEM_BYTES = 67_000_000
NEG = -1e30

PIECE = 128
QT = 256


def rope_tables(positions, head_dim):
    inv_freq = 1.0 / (ROPE_BASE ** (jnp.arange(0, head_dim, 2, dtype=F32) / head_dim))
    angles = positions.astype(F32)[:, None] * inv_freq[None, :]
    return jnp.cos(angles), jnp.sin(angles)


def _block_of(me, slot):
    chip = lax.rem(me // 2 + slot // 2, 2)
    core = lax.rem(lax.rem(me, 2) + lax.rem(slot, 2), 2)
    return chip * 2 + core


def attention_kernel(rows, heads, head_dim, x_hbm, g_ref, w_hbm, cos_ref, sin_ref, o_hbm,
                     xb, w, q_buf, k_buf, v_buf, xn, m_ref, l_ref, acc,
                     x_sem, w_sem, psend, precv, csend, crecv, dsend, drecv, osend, orecv, olocal):
    me = lax.axis_index('seq')
    hl = heads // 4
    n_chunks = rows // PIECE
    inner = heads * head_dim

    def w_copy(t, h):
        col = pl.multiple_of(t * inner + (me * hl + h) * head_dim, head_dim)
        return pltpu.make_async_copy(w_hbm.at[:, pl.ds(col, head_dim)], w.at[t * hl + h], w_sem.at[t * hl + h])

    x_local = pltpu.make_async_copy(x_hbm, xb.at[0], x_sem)
    x_local.start()
    for h in range(hl):
        for t in range(3):
            w_copy(t, h).start()

    barrier = pltpu.get_barrier_semaphore()
    for slot in (1, 2, 3):
        pl.semaphore_signal(barrier, inc=1, device_id={'seq': _block_of(me, slot)}, device_id_type=pl.DeviceIdType.MESH)
    pl.semaphore_wait(barrier, 3)

    def cross_copy(c):
        rs = pl.ds(c * PIECE, PIECE)
        return pltpu.make_async_remote_copy(
            src_ref=x_hbm.at[rs], dst_ref=xb.at[2, rs], send_sem=csend.at[c], recv_sem=crecv.at[c],
            device_id={'seq': _block_of(me, 2)}, device_id_type=pl.DeviceIdType.MESH)

    def diag_copy(c):
        rs = pl.ds(c * PIECE, PIECE)
        return pltpu.make_async_remote_copy(
            src_ref=xb.at[2, rs], dst_ref=xb.at[3, rs], send_sem=dsend.at[c], recv_sem=drecv.at[c],
            device_id={'seq': _block_of(me, 1)}, device_id_type=pl.DeviceIdType.MESH)

    partner = pltpu.make_async_remote_copy(
        src_ref=x_hbm, dst_ref=xb.at[1], send_sem=psend, recv_sem=precv,
        device_id={'seq': _block_of(me, 1)}, device_id_type=pl.DeviceIdType.MESH)
    for c in range(n_chunks):
        cross_copy(c).start()
    partner.start()
    x_local.wait()

    def project(j, slot, row, first):
        xf = xb[slot, pl.ds(row, PIECE), :].astype(F32)
        inv = lax.rsqrt(jnp.mean(xf * xf, axis=-1, keepdims=True) + 1e-5)
        xn[...] = (xf * inv * g_ref[...]).astype(BF16)
        base = pl.multiple_of(_block_of(me, slot) * rows + row, PIECE)
        cos_t = cos_ref[pl.ds(base, PIECE), :]
        sin_t = sin_ref[pl.ds(base, PIECE), :]
        half = head_dim // 2

        def one_head(h, _):
            for t, dst in ((0, q_buf), (1, k_buf), (2, v_buf)):
                @pl.when(j == 0)
                def _():
                    w_copy(t, h).wait()
                u = jnp.dot(xn[...], w[t * hl + h], preferred_element_type=F32)
                if t < 2:
                    a, b = u[:, :half], u[:, half:]
                    dst[h, pl.ds(base, PIECE), :half] = (a * cos_t - b * sin_t).astype(BF16)
                    dst[h, pl.ds(base, PIECE), half:] = (b * cos_t + a * sin_t).astype(BF16)
                else:
                    dst[h, pl.ds(base, PIECE), :] = u.astype(BF16)
            return 0
        lax.fori_loop(0, hl, one_head, 0)

    def piece(j, _):
        c = lax.rem(j, n_chunks)
        late = j // (2 * n_chunks)
        jj = j - 2 * n_chunks
        slot = (1 - late) * (j // n_chunks) + late * (2 + lax.rem(jj, 2))
        chunk = (1 - late) * c + late * (jj // 2)
        row = pl.multiple_of(chunk * PIECE, PIECE)

        @pl.when(j == n_chunks)
        def _():
            partner.wait_recv()

        @pl.when(slot == 2)
        def _():
            cross_copy(chunk).wait_recv()
            diag_copy(chunk).start()

        @pl.when(slot == 3)
        def _():
            diag_copy(chunk).wait_recv()

        project(j, slot, row, False)
        return 0

    lax.fori_loop(0, 4 * n_chunks, piece, 0)

    tiles = rows // QT
    scale = (head_dim ** -0.5) * LOG2E

    def unit(u):
        i = u // (2 * tiles)
        slot = (i + 2) * (1 - i // 2) + (3 - i) * (i // 2)
        tile = lax.rem(u // 2, tiles)
        hp = lax.rem(u, 2)
        return slot, tile, hp

    def out_remote(slot, tile, h):
        dst_block = _block_of(me, slot)
        src_row = pl.multiple_of(dst_block * rows + tile * QT, QT)
        col = pl.multiple_of((me * hl + h) * head_dim, head_dim)
        return pltpu.make_async_remote_copy(
            src_ref=q_buf.at[h, pl.ds(src_row, QT), :],
            dst_ref=o_hbm.at[pl.ds(pl.multiple_of(tile * QT, QT), QT), pl.ds(col, head_dim)],
            send_sem=osend.at[slot, tile, h], recv_sem=orecv.at[slot, tile, h],
            device_id={'seq': dst_block}, device_id_type=pl.DeviceIdType.MESH)

    def out_local(tile, h):
        src_row = pl.multiple_of(me * rows + tile * QT, QT)
        col = pl.multiple_of((me * hl + h) * head_dim, head_dim)
        return pltpu.make_async_copy(
            q_buf.at[h, pl.ds(src_row, QT), :],
            o_hbm.at[pl.ds(pl.multiple_of(tile * QT, QT), QT), pl.ds(col, head_dim)],
            olocal.at[tile, h])

    def send_unit(u):
        slot, tile, hp = unit(u)
        for d in range(2):
            h = hp * 2 + d

            @pl.when(slot > 0)
            def _():
                out_remote(slot, tile, h).start()

            @pl.when(slot == 0)
            def _():
                out_local(tile, h).start()

    def attend(u, _):
        slot, tile, hp = unit(u)
        block = _block_of(me, slot)
        qrow = pl.multiple_of(block * rows + tile * QT, QT)

        def scores(d, kc):
            h = hp * 2 + d
            kk = k_buf[h, pl.ds(pl.multiple_of(kc * rows, rows), rows), :]
            return lax.dot_general(q_buf[h, pl.ds(qrow, QT), :], kk, (((1,), (1,)), ((), ())), preferred_element_type=F32)

        def lane_sum(p):
            s = p[:, :128]
            for i in range(1, rows // 128):
                s = s + p[:, i * 128:(i + 1) * 128]
            return s

        for d in range(2):
            h = hp * 2 + d
            s = scores(d, block)
            ri = lax.broadcasted_iota(jnp.int32, (QT, rows), 0) + tile * QT
            ci = lax.broadcasted_iota(jnp.int32, (QT, rows), 1)
            s = jnp.where(ci <= ri, s, NEG)
            m = jnp.max(s, axis=-1, keepdims=True)
            p = jnp.exp2((s - m) * scale)
            m_ref[d] = jnp.broadcast_to(m, (QT, 128))
            l_ref[d] = lane_sum(p)
            vv = v_buf[h, pl.ds(pl.multiple_of(block * rows, rows), rows), :]
            acc[d] = jnp.dot(p.astype(BF16), vv, preferred_element_type=F32)

        def earlier(kc, _):
            for d in range(2):
                h = hp * 2 + d
                s = scores(d, kc)
                m_old = m_ref[d][:, :1]
                m = jnp.maximum(m_old, jnp.max(s, axis=-1, keepdims=True))
                alpha = jnp.exp2((m_old - m) * scale)
                p = jnp.exp2((s - m) * scale)
                m_ref[d] = jnp.broadcast_to(m, (QT, 128))
                l_ref[d] = l_ref[d] * alpha + lane_sum(p)
                vv = v_buf[h, pl.ds(pl.multiple_of(kc * rows, rows), rows), :]
                acc[d] = acc[d] * alpha + jnp.dot(p.astype(BF16), vv, preferred_element_type=F32)
            return 0
        lax.fori_loop(0, block, earlier, 0)

        for d in range(2):
            h = hp * 2 + d
            denom = jnp.sum(l_ref[d], axis=-1, keepdims=True)
            q_buf[h, pl.ds(qrow, QT), :] = (acc[d] / denom).astype(BF16)

        @pl.when(u > 0)
        def _():
            send_unit(u - 1)
        return 0

    n_units = 4 * tiles * 2
    lax.fori_loop(0, n_units, attend, 0)
    send_unit(n_units - 1)

    partner.wait_send()
    for c in range(n_chunks):
        cross_copy(c).wait_send()
        diag_copy(c).wait_send()
    for tile in range(tiles):
        for h in range(hl):
            out_local(tile, h).wait()
            for slot in (1, 2, 3):
                out_remote(slot, tile, h).wait_send()
                out_remote(slot, tile, h).wait_recv()


def attention(x_blk, g_attn, w_qkv, heads, head_dim):
    rows, width = x_blk.shape
    seq = 4 * rows
    hl = heads // 4
    n_chunks = rows // PIECE
    tiles = rows // QT
    cos_tab, sin_tab = rope_tables(jnp.arange(seq), head_dim)
    dma = pltpu.SemaphoreType.DMA
    anys = pl.BlockSpec(memory_space=pl.ANY)
    vm = pl.BlockSpec(memory_space=pltpu.VMEM)
    return pl.pallas_call(
        functools.partial(attention_kernel, rows, heads, head_dim),
        out_shape=jax.ShapeDtypeStruct((rows, heads * head_dim), BF16),
        in_specs=[anys, vm, anys, vm, vm],
        out_specs=anys,
        scratch_shapes=[
            pltpu.VMEM((4, rows, width), BF16),
            pltpu.VMEM((3 * hl, width, head_dim), BF16),
            pltpu.VMEM((hl, seq, head_dim), BF16),
            pltpu.VMEM((hl, seq, head_dim), BF16),
            pltpu.VMEM((hl, seq, head_dim), BF16),
            pltpu.VMEM((PIECE, width), BF16),
            pltpu.VMEM((2, QT, 128), F32),
            pltpu.VMEM((2, QT, 128), F32),
            pltpu.VMEM((2, QT, head_dim), F32),
            dma, dma((3 * hl,)), dma, dma,
            dma((n_chunks,)), dma((n_chunks,)), dma((n_chunks,)), dma((n_chunks,)),
            dma((4, tiles, hl)), dma((4, tiles, hl)), dma((tiles, hl)),
        ],
        compiler_params=pltpu.CompilerParams(
            collective_id=0, has_side_effects=True, vmem_limit_bytes=VMEM_BYTES),
        name='gather_attention',
    )(x_blk, g_attn.reshape(1, width), w_qkv, cos_tab, sin_tab)


def mlp_kernel(n_out, n_ff, bn, o_ref, x_ref, wo_ref, gm_ref, wg_ref, wu_ref, wd_ref, z_ref, acc, yn):
    i = pl.program_id(0)

    for s in range(n_out):
        @pl.when(i == s)
        def _():
            mixed = jnp.dot(o_ref[...], wo_ref[...], preferred_element_type=F32)
            y = (x_ref[...].astype(F32) + mixed).astype(BF16)
            acc[:, s * bn:(s + 1) * bn] = y.astype(F32)

    @pl.when(i == n_out)
    def _():
        y = acc[...]
        inv = lax.rsqrt(jnp.mean(y * y, axis=-1, keepdims=True) + 1e-5)
        yn[...] = (y * inv * gm_ref[...]).astype(BF16)

    @pl.when(i >= n_out)
    def _():
        gate = jnp.dot(yn[...], wg_ref[...], preferred_element_type=F32)
        up = jnp.dot(yn[...], wu_ref[...], preferred_element_type=F32)
        hidden = (gate * jax.nn.sigmoid(gate) * up).astype(BF16)
        width = acc.shape[1]
        step = width // 4
        for j in range(4):
            cs = slice(j * step, (j + 1) * step)
            acc[:, cs] += jnp.dot(hidden, wd_ref[:, cs], preferred_element_type=F32)

    @pl.when(i == n_out + n_ff - 1)
    def _():
        z_ref[...] = acc[...].astype(BF16)


def out_and_mlp(attn_rows, x_blk, w_out, g_mlp, w_gate, w_up, w_down):
    rows, width = x_blk.shape
    inner = attn_rows.shape[1]
    ff = w_gate.shape[1]
    bn = 512
    bf = 512
    n_out = width // bn
    n_ff = ff // bf
    one = pl.Buffered(1)
    c0 = lambda i: (0, 0)
    ffi = lambda i: jnp.maximum(i - n_out, 0)
    return pl.pallas_call(
        functools.partial(mlp_kernel, n_out, n_ff, bn),
        grid=(n_out + n_ff,),
        in_specs=[
            pl.BlockSpec((rows, inner), c0, pipeline_mode=one),
            pl.BlockSpec((rows, bn), lambda i: (0, jnp.minimum(i, n_out - 1))),
            pl.BlockSpec((inner, bn), lambda i: (0, jnp.minimum(i, n_out - 1))),
            pl.BlockSpec((1, width), c0, pipeline_mode=one),
            pl.BlockSpec((width, bf), lambda i: (0, ffi(i))),
            pl.BlockSpec((width, bf), lambda i: (0, ffi(i))),
            pl.BlockSpec((bf, width), lambda i: (ffi(i), 0)),
        ],
        out_specs=pl.BlockSpec((rows, width), c0, pipeline_mode=one),
        out_shape=jax.ShapeDtypeStruct((rows, width), BF16),
        scratch_shapes=[pltpu.VMEM((rows, width), F32), pltpu.VMEM((rows, width), BF16)],
        compiler_params=pltpu.CompilerParams(
            dimension_semantics=('arbitrary',), vmem_limit_bytes=VMEM_BYTES),
        name='out_mlp',
    )(attn_rows, x_blk, w_out, g_mlp.reshape(1, width), w_gate, w_up, w_down)


def solution(mesh):
    def local_layer(x_blk, g_attn, w_qkv, w_out, g_mlp, w_gate, w_up, w_down):
        n_heads, head_dim, model_width = w_out.shape
        attn_rows = attention(x_blk, g_attn, w_qkv, n_heads, head_dim)
        return out_and_mlp(attn_rows, x_blk, w_out.reshape(n_heads * head_dim, model_width), g_mlp, w_gate, w_up, w_down)

    row_spec = P(('data', 'seq'), None)
    return jax.shard_map(local_layer, mesh=mesh, in_specs=(row_spec, P(), P(), P(), P(), P(), P(), P()), out_specs=row_spec, check_vma=False)
```

time: 754 us -> 447 us (0.59)
  Pallas kernels: 0 us -> 441 us
  matrix products: 418 us -> 0 us
  waiting for transfers between devices: 139 us -> 0 us
  local copies, waits for them, and re-layouts: 87.3 us -> 0 us
  blocking collectives: 51.2 us -> 0 us
  other arithmetic: 41.2 us -> 5.55 us
    pallas_call x0 -> x2, Pallas kernels: none -> 441 us  [the longest x1 251 us: out_and_mlp(): pl.pallas_call(functools.partial(mlp_kernel, n_out, n_ff, bn), grid=(n_ou...]
    dot_general x9 -> x0, matrix products: 374 us -> none  [the longest x1 82.2 us: gated_mlp(): jnp.dot(hidden, w_down, preferred_element_type=jnp.float32)]
    all_to_all x1 -> x0, waiting for transfers between devices: 139 us -> none  [local_layer(): head_major = lax.all_to_all(packed, 'seq', 2, 0, tiled=True)]
    all_to_all x1 -> x0, blocking collectives: 51.2 us -> none  [local_layer(): attn_rows = lax.all_to_all(attn_heads, 'seq', 0, 1, tiled=True)]
    sub x4 -> x0, matrix products: 43.9 us -> none  [one_block(): attn_probs = jax.nn.softmax(scores, axis=-1).astype(jnp.bfloat16)]
    unnamed x7 -> x0, local copies, waits for them, and re-layouts: 34.9 us -> none
    slice x3 -> x0, local copies, waits for them, and re-layouts: 23.4 us -> none  [the longest x1 12.3 us: local_layer(): qkv_f32[:, :2]]
    another operation x1 -> x0, other arithmetic: 17.6 us -> none
  transfers between devices with their start and end apart: 1 -> 0, of which waited for: 1 -> 0; matrix products, arithmetic and copies ran while one was open for 0% -> 0% of each run, Pallas kernels for 0% -> 0%
where the time goes in v1:
time: 447 us; the launch traced here: 446 us
  Pallas kernels  441 us (99%)
  other arithmetic  5.55 us (1%)
    pallas_call x1, Pallas kernels, out_and_mlp(): pl.pallas_call(functools.partial(mlp_kernel, n_out, n_ff, bn), grid=(n_ou...  251 us
    pallas_call x1, Pallas kernels, attention(): pl.pallas_call(functools.partial(attention_kernel, rows, heads, head_dim)...  190 us

profile of v1, /device:TPU:0, one launch (start us, length us, event | category | flops | bytes accessed | tf_op | source)
XLA Modules:
  0.0 446.2 jit_solution(5438500751747984776)
XLA Ops:
  0.0 5.5 %multiply_sine_fusion = (f32[2048,128]{1,0:T(8,128)}, f32[2048,128]{1,0:T(8,128)}) fusion(f32[128]{0:T(128)S(1)} %negate_power_fusion, f32[2048]{0:T(1024)S(1)} %iota_convert_fusion), kind=kLoop, calls=%fused_computation | loop fusion | flops 262144 | bytes 2105856 | tf_op jit(solution)/shard_map/sin | solution.py:24
  5.6 190.0 %gather_attention.1.o_ref = bf16[512,4096]{1,0:T(8,128)(2,1)} custom-call(bf16[512,4096]{1,0:T(8,128)(2,1)} %x_ref.1, f32[1,4096]{1,0:T(1,128)} %bitcast.4, bf16[4096,12288]{1,0:T(8,128)(2,1)} %w_hbm.1, f32[2048,128]{1,0:T(8,128)} %get-tuple-element.6.cos_ref, f32[2048,128]{1,0:T(8,128)} %get-tuple-element.5.sin_ref), custom_call_target="tpu_custom_call" | custom-call | tf_op jit(solution)/shard_map/gather_attention/pallas_call | solution.py:247
  195.6 250.6 %out_mlp.1 = bf16[512,4096]{1,0:T(8,128)(2,1)} custom-call(bf16[512,4096]{1,0:T(8,128)(2,1)} %gather_attention.1.o_ref, bf16[512,4096]{1,0:T(8,128)(2,1)} %x_ref.1, bf16[4096,4096]{1,0:T(8,128)(2,1)} %bitcast.3, f32[1,4096]{1,0:T(1,128)} %bitcast.5, bf16[4096,16384]{1,0:T(8,128)(2,1)} %wg_ref.1, bf16[4096,16384]{1,0:T(8,128)(2,1)} %wu_ref.1, ...), custom_call_target="tpu_custom_call" | custom-call | tf_op jit(solution)/shard_map/out_mlp/pallas_call | solution.py:315
  (2 shorter events, 0.0 us)

commit v2 on v1

--- a/solution.py
+++ b/solution.py
@@ -15,11 +15,13 @@
 NEG = -1e30
 
 PIECE = 128
+CHUNK = 64
 QT = 256
 
 
-def rope_tables(positions, head_dim):
+def rope_tables(seq, head_dim):
     inv_freq = 1.0 / (ROPE_BASE ** (jnp.arange(0, head_dim, 2, dtype=F32) / head_dim))
+    positions = jnp.concatenate([jnp.arange(PIECE), jnp.arange(0, seq, PIECE)])
     angles = positions.astype(F32)[:, None] * inv_freq[None, :]
     return jnp.cos(angles), jnp.sin(angles)
 
@@ -31,11 +33,13 @@
 
 
 def attention_kernel(rows, heads, head_dim, x_hbm, g_ref, w_hbm, cos_ref, sin_ref, o_hbm,
-                     xb, w, q_buf, k_buf, v_buf, xn, m_ref, l_ref, acc,
+                     xb, w, q_buf, k_buf, v_buf, xn, tab, m_ref, l_ref, acc,
                      x_sem, w_sem, psend, precv, csend, crecv, dsend, drecv, osend, orecv, olocal):
     me = lax.axis_index('seq')
     hl = heads // 4
-    n_chunks = rows // PIECE
+    n_pieces = rows // PIECE
+    n_chunks = rows // CHUNK
+    core = lax.rem(me, 2)
     inner = heads * head_dim
 
     def w_copy(t, h):
@@ -44,9 +48,8 @@
 
     x_local = pltpu.make_async_copy(x_hbm, xb.at[0], x_sem)
     x_local.start()
-    for h in range(hl):
-        for t in range(3):
-            w_copy(t, h).start()
+    for t in range(3):
+        w_copy(t, 0).start()
 
     barrier = pltpu.get_barrier_semaphore()
     for slot in (1, 2, 3):
@@ -54,13 +57,13 @@
     pl.semaphore_wait(barrier, 3)
 
     def cross_copy(c):
-        rs = pl.ds(c * PIECE, PIECE)
+        rs = pl.ds(pl.multiple_of(c * CHUNK, CHUNK), CHUNK)
         return pltpu.make_async_remote_copy(
             src_ref=x_hbm.at[rs], dst_ref=xb.at[2, rs], send_sem=csend.at[c], recv_sem=crecv.at[c],
             device_id={'seq': _block_of(me, 2)}, device_id_type=pl.DeviceIdType.MESH)
 
     def diag_copy(c):
-        rs = pl.ds(c * PIECE, PIECE)
+        rs = pl.ds(pl.multiple_of(c * CHUNK, CHUNK), CHUNK)
         return pltpu.make_async_remote_copy(
             src_ref=xb.at[2, rs], dst_ref=xb.at[3, rs], send_sem=dsend.at[c], recv_sem=drecv.at[c],
             device_id={'seq': _block_of(me, 1)}, device_id_type=pl.DeviceIdType.MESH)
@@ -68,67 +71,97 @@
     partner = pltpu.make_async_remote_copy(
         src_ref=x_hbm, dst_ref=xb.at[1], send_sem=psend, recv_sem=precv,
         device_id={'seq': _block_of(me, 1)}, device_id_type=pl.DeviceIdType.MESH)
-    for c in range(n_chunks):
-        cross_copy(c).start()
+    cross_copy(0).start()
     partner.start()
     x_local.wait()
-
-    def project(j, slot, row, first):
-        xf = xb[slot, pl.ds(row, PIECE), :].astype(F32)
-        inv = lax.rsqrt(jnp.mean(xf * xf, axis=-1, keepdims=True) + 1e-5)
-        xn[...] = (xf * inv * g_ref[...]).astype(BF16)
-        base = pl.multiple_of(_block_of(me, slot) * rows + row, PIECE)
-        cos_t = cos_ref[pl.ds(base, PIECE), :]
-        sin_t = sin_ref[pl.ds(base, PIECE), :]
-        half = head_dim // 2
+    for h in range(1, hl):
+        for t in range(3):
+            w_copy(t, h).start()
+
+    def norm_rows(slot, row, count, at):
+        width = g_ref.shape[1]
+        cw = 1024
+        for r in range(0, count, 16):
+            rs = pl.ds(pl.multiple_of(row + r, 16), 16)
+            total = jnp.zeros((16, 128), F32)
+            for c in range(0, width, cw):
+                xf = xb[slot, rs, c:c + cw].astype(F32)
+                sq = xf * xf
+                for i in range(0, cw, 128):
+                    total = total + sq[:, i:i + 128]
+            inv = lax.rsqrt(jnp.sum(total, axis=-1, keepdims=True) / width + 1e-5)
+            for c in range(0, width, cw):
+                xf = xb[slot, rs, c:c + cw].astype(F32)
+                xn[at + r:at + r + 16, c:c + cw] = (xf * inv * g_ref[:, c:c + cw]).astype(BF16)
+
+    half = head_dim // 2
+
+    def project(first, bases):
+        run = PIECE // len(bases)
+        tabs = []
+        for i, base in enumerate(bases):
+            low = lax.rem(base, PIECE)
+            c0 = cos_ref[pl.ds(pl.multiple_of(low, run), run), :]
+            s0 = sin_ref[pl.ds(pl.multiple_of(low, run), run), :]
+            c1 = cos_ref[pl.ds(PIECE + base // PIECE, 1), :]
+            s1 = sin_ref[pl.ds(PIECE + base // PIECE, 1), :]
+            tabs.append((c0 * c1 - s0 * s1, s0 * c1 + c0 * s1))
+        cos_t = jnp.concatenate([t[0] for t in tabs], axis=0)
+        sin_t = jnp.concatenate([t[1] for t in tabs], axis=0)
+        tab[0] = cos_t
+        tab[1] = sin_t
 
         def one_head(h, _):
+            if first is not None:
+                @pl.when(first)
+                def _():
+                    for t in range(3):
+                        w_copy(t, h).wait()
             for t, dst in ((0, q_buf), (1, k_buf), (2, v_buf)):
-                @pl.when(j == 0)
-                def _():
-                    w_copy(t, h).wait()
                 u = jnp.dot(xn[...], w[t * hl + h], preferred_element_type=F32)
                 if t < 2:
                     a, b = u[:, :half], u[:, half:]
-                    dst[h, pl.ds(base, PIECE), :half] = (a * cos_t - b * sin_t).astype(BF16)
-                    dst[h, pl.ds(base, PIECE), half:] = (b * cos_t + a * sin_t).astype(BF16)
+                    parts = ((0, (a * tab[0] - b * tab[1]).astype(BF16)), (half, (b * tab[0] + a * tab[1]).astype(BF16)))
                 else:
-                    dst[h, pl.ds(base, PIECE), :] = u.astype(BF16)
+                    parts = ((0, u.astype(BF16)),)
+                for off, val in parts:
+                    for i, base in enumerate(bases):
+                        dst[h, pl.ds(pl.multiple_of(base, run), run), off:off + val.shape[1]] = val[i * run:(i + 1) * run]
             return 0
         lax.fori_loop(0, hl, one_head, 0)
 
-    def piece(j, _):
-        c = lax.rem(j, n_chunks)
-        late = j // (2 * n_chunks)
-        jj = j - 2 * n_chunks
-        slot = (1 - late) * (j // n_chunks) + late * (2 + lax.rem(jj, 2))
-        chunk = (1 - late) * c + late * (jj // 2)
-        row = pl.multiple_of(chunk * PIECE, PIECE)
-
-        @pl.when(j == n_chunks)
+    def near_piece(j, _):
+        slot = j // n_pieces
+        row = pl.multiple_of(lax.rem(j, n_pieces) * PIECE, PIECE)
+
+        @pl.when(j == n_pieces)
         def _():
             partner.wait_recv()
 
-        @pl.when(slot == 2)
-        def _():
-            cross_copy(chunk).wait_recv()
-            diag_copy(chunk).start()
-
-        @pl.when(slot == 3)
-        def _():
-            diag_copy(chunk).wait_recv()
-
-        project(j, slot, row, False)
+        norm_rows(slot, row, PIECE, 0)
+        project(j == 0, [_block_of(me, slot) * rows + row])
+
+        @pl.when(j == 0)
+        def _():
+            cross_copy(1).start()
+
+        @pl.when((j >= 3) & (lax.rem(j, 2) == 1))
+        def _():
+            done = (j - 3) // 2
+            cross_copy(done).wait_send()
+            cross_copy(done + 2).start()
         return 0
 
-    lax.fori_loop(0, 4 * n_chunks, piece, 0)
+    lax.fori_loop(0, 2 * n_pieces, near_piece, 0)
+    n_near = n_pieces - 1
 
     tiles = rows // QT
     scale = (head_dim ** -0.5) * LOG2E
 
     def unit(u):
         i = u // (2 * tiles)
-        slot = (i + 2) * (1 - i // 2) + (3 - i) * (i // 2)
+        far = 2 + lax.rem(i + core, 2)
+        slot = far * (1 - i // 2) + (3 - i) * (i // 2)
         tile = lax.rem(u // 2, tiles)
         hp = lax.rem(u, 2)
         return slot, tile, hp
@@ -164,67 +197,107 @@
             def _():
                 out_local(tile, h).start()
 
-    def attend(u, _):
+    def attend(u):
         slot, tile, hp = unit(u)
         block = _block_of(me, slot)
-        qrow = pl.multiple_of(block * rows + tile * QT, QT)
-
-        def scores(d, kc):
+        first = pl.multiple_of(block * rows, rows)
+        qrow = pl.multiple_of(first + tile * QT, QT)
+
+        def scores(d, row, count):
             h = hp * 2 + d
-            kk = k_buf[h, pl.ds(pl.multiple_of(kc * rows, rows), rows), :]
+            kk = k_buf[h, pl.ds(row, count), :]
             return lax.dot_general(q_buf[h, pl.ds(qrow, QT), :], kk, (((1,), (1,)), ((), ())), preferred_element_type=F32)
 
         def lane_sum(p):
             s = p[:, :128]
-            for i in range(1, rows // 128):
-                s = s + p[:, i * 128:(i + 1) * 128]
+            for i in range(128, p.shape[1], 128):
+                s = s + p[:, i:i + 128]
             return s
 
         for d in range(2):
             h = hp * 2 + d
-            s = scores(d, block)
-            ri = lax.broadcasted_iota(jnp.int32, (QT, rows), 0) + tile * QT
-            ci = lax.broadcasted_iota(jnp.int32, (QT, rows), 1)
+            s = scores(d, qrow, QT)
+            ri = lax.broadcasted_iota(jnp.int32, (QT, QT), 0)
+            ci = lax.broadcasted_iota(jnp.int32, (QT, QT), 1)
             s = jnp.where(ci <= ri, s, NEG)
             m = jnp.max(s, axis=-1, keepdims=True)
             p = jnp.exp2((s - m) * scale)
             m_ref[d] = jnp.broadcast_to(m, (QT, 128))
             l_ref[d] = lane_sum(p)
-            vv = v_buf[h, pl.ds(pl.multiple_of(block * rows, rows), rows), :]
-            acc[d] = jnp.dot(p.astype(BF16), vv, preferred_element_type=F32)
-
-        def earlier(kc, _):
+            acc[d] = jnp.dot(p.astype(BF16), v_buf[h, pl.ds(qrow, QT), :], preferred_element_type=F32)
+
+        def update(row, count):
             for d in range(2):
                 h = hp * 2 + d
-                s = scores(d, kc)
+                s = scores(d, row, count)
                 m_old = m_ref[d][:, :1]
                 m = jnp.maximum(m_old, jnp.max(s, axis=-1, keepdims=True))
                 alpha = jnp.exp2((m_old - m) * scale)
                 p = jnp.exp2((s - m) * scale)
                 m_ref[d] = jnp.broadcast_to(m, (QT, 128))
                 l_ref[d] = l_ref[d] * alpha + lane_sum(p)
-                vv = v_buf[h, pl.ds(pl.multiple_of(kc * rows, rows), rows), :]
-                acc[d] = acc[d] * alpha + jnp.dot(p.astype(BF16), vv, preferred_element_type=F32)
+                acc[d] = acc[d] * alpha + jnp.dot(p.astype(BF16), v_buf[h, pl.ds(row, count), :], preferred_element_type=F32)
+
+        def earlier_tile(kt, _):
+            update(pl.multiple_of(first + kt * QT, QT), QT)
             return 0
-        lax.fori_loop(0, block, earlier, 0)
+        lax.fori_loop(0, tile, earlier_tile, 0)
+
+        def earlier_block(kb, _):
+            update(pl.multiple_of(kb * rows, rows), rows)
+            return 0
+        lax.fori_loop(0, block, earlier_block, 0)
 
         for d in range(2):
             h = hp * 2 + d
             denom = jnp.sum(l_ref[d], axis=-1, keepdims=True)
             q_buf[h, pl.ds(qrow, QT), :] = (acc[d] / denom).astype(BF16)
 
-        @pl.when(u > 0)
-        def _():
-            send_unit(u - 1)
+    early = rows // CHUNK // tiles
+    n_early = 2
+    n_units = 4 * tiles * 2
+
+    def far_step(i, _):
+        is_unit = ((i >= early) & (i < early + n_early)) | (i >= n_chunks + n_early)
+
+        @pl.when(jnp.logical_not(is_unit))
+        def _():
+            k = i - n_early * ((i >= early).astype(jnp.int32))
+            cross_copy(k).wait_recv()
+            diag_copy(k).start()
+
+            @pl.when((k >= n_near) & (k < n_chunks - 2))
+            def _():
+                cross_copy(k).wait_send()
+                cross_copy(k + 2).start()
+
+            @pl.when(k == n_chunks - 1)
+            def _():
+                for u in range(n_early):
+                    send_unit(u)
+            row = pl.multiple_of(k * CHUNK, CHUNK)
+            norm_rows(2, row, CHUNK, 0)
+            diag_copy(k).wait_recv()
+            norm_rows(3, row, CHUNK, CHUNK)
+            project(None, [_block_of(me, 2) * rows + row, _block_of(me, 3) * rows + row])
+
+        @pl.when(is_unit)
+        def _():
+            u = i - early * (1 - (i >= n_chunks + n_early).astype(jnp.int32)) - n_chunks * ((i >= n_chunks + n_early).astype(jnp.int32))
+            attend(u)
+
+            @pl.when(u > n_early)
+            def _():
+                send_unit(u - 1)
         return 0
 
-    n_units = 4 * tiles * 2
-    lax.fori_loop(0, n_units, attend, 0)
+    lax.fori_loop(0, n_chunks + n_units, far_step, 0)
     send_unit(n_units - 1)
 
     partner.wait_send()
     for c in range(n_chunks):
-        cross_copy(c).wait_send()
+        if c >= n_chunks - 2:
+            cross_copy(c).wait_send()
         diag_copy(c).wait_send()
     for tile in range(tiles):
         for h in range(hl):
@@ -238,9 +311,9 @@
     rows, width = x_blk.shape
     seq = 4 * rows
     hl = heads // 4
-    n_chunks = rows // PIECE
+    n_chunks = rows // CHUNK
     tiles = rows // QT
-    cos_tab, sin_tab = rope_tables(jnp.arange(seq), head_dim)
+    cos_tab, sin_tab = rope_tables(seq, head_dim)
     dma = pltpu.SemaphoreType.DMA
     anys = pl.BlockSpec(memory_space=pl.ANY)
     vm = pl.BlockSpec(memory_space=pltpu.VMEM)
@@ -256,6 +329,7 @@
             pltpu.VMEM((hl, seq, head_dim), BF16),
             pltpu.VMEM((hl, seq, head_dim), BF16),
             pltpu.VMEM((PIECE, width), BF16),
+            pltpu.VMEM((2, PIECE, head_dim // 2), F32),
             pltpu.VMEM((2, QT, 128), F32),
             pltpu.VMEM((2, QT, 128), F32),
             pltpu.VMEM((2, QT, head_dim), F32),
@@ -281,9 +355,22 @@
 
     @pl.when(i == n_out)
     def _():
-        y = acc[...]
-        inv = lax.rsqrt(jnp.mean(y * y, axis=-1, keepdims=True) + 1e-5)
-        yn[...] = (y * inv * gm_ref[...]).astype(BF16)
+        n_rows, width = acc.shape
+        cw = 1024
+
+        def slab(r, _):
+            rs = pl.ds(pl.multiple_of(r * 32, 32), 32)
+            total = jnp.zeros((32, 128), F32)
+            for c in range(0, width, cw):
+                y = acc[rs, c:c + cw]
+                sq = y * y
+                for k in range(0, cw, 128):
+                    total = total + sq[:, k:k + 128]
+            inv = lax.rsqrt(jnp.sum(total, axis=-1, keepdims=True) / width + 1e-5)
+            for c in range(0, width, cw):
+                yn[rs, c:c + cw] = (acc[rs, c:c + cw] * inv * gm_ref[:, c:c + cw]).astype(BF16)
+            return 0
+        lax.fori_loop(0, n_rows // 32, slab, 0, unroll=2)
 
     @pl.when(i >= n_out)
     def _():

time: 447 us -> 400 us (0.89)
  Pallas kernels: 441 us -> 399 us
  other arithmetic: 5.55 us -> 1.03 us
    pallas_call x1, Pallas kernels: 190 us -> 148 us  [attention(): pl.pallas_call(functools.partial(attention_kernel, rows, heads, head_dim)...]
    sin x1, other arithmetic: 5.54 us -> 1.01 us  [rope_tables(): return (jnp.cos(angles), jnp.sin(angles))]
where the time goes in v2:
time: 400 us
  Pallas kernels  399 us (100%)
    pallas_call x1, Pallas kernels, out_and_mlp(): pl.pallas_call(functools.partial(mlp_kernel, n_out, n_ff, bn), grid=(n_ou...  250 us
    pallas_call x1, Pallas kernels, attention(): pl.pallas_call(functools.partial(attention_kernel, rows, heads, head_dim)...  148 us

profile of v2, /device:TPU:0, one launch (start us, length us, event | category | flops | bytes accessed | tf_op | source)
XLA Modules:
  0.0 399.7 jit_solution(11951012814654770171)
XLA Ops:
  0.0 1.0 multiply_sine_fusion
  1.0 148.3 %gather_attention.1.o_ref = bf16[512,4096]{1,0:T(8,128)(2,1)} custom-call(bf16[512,4096]{1,0:T(8,128)(2,1)} %x_ref.1, f32[1,4096]{1,0:T(1,128)} %bitcast.4, bf16[4096,12288]{1,0:T(8,128)(2,1)} %w_hbm.1, f32[144,128]{1,0:T(8,128)} %get-tuple-element.6.cos_ref, f32[144,128]{1,0:T(8,128)} %get-tuple-element.5.sin_ref), custom_call_target="tpu_custom_call" | custom-call | tf_op jit(solution)/shard_map/gather_attention/pallas_call | solution.py:320
  149.3 250.3 %out_mlp.1 = bf16[512,4096]{1,0:T(8,128)(2,1)} custom-call(bf16[512,4096]{1,0:T(8,128)(2,1)} %gather_attention.1.o_ref, bf16[512,4096]{1,0:T(8,128)(2,1)} %x_ref.1, bf16[4096,4096]{1,0:T(8,128)(2,1)} %bitcast.3, f32[1,4096]{1,0:T(1,128)} %bitcast.5, bf16[4096,16384]{1,0:T(8,128)(2,1)} %wg_ref.1, bf16[4096,16384]{1,0:T(8,128)(2,1)} %wu_ref.1, ...), custom_call_target="tpu_custom_call" | custom-call | tf_op jit(solution)/shard_map/out_mlp/pallas_call | solution.py:402
  (4 shorter events, 0.0 us)

commit v3 on v2

--- a/solution.py
+++ b/solution.py
@@ -206,37 +206,34 @@
         def scores(d, row, count):
             h = hp * 2 + d
             kk = k_buf[h, pl.ds(row, count), :]
-            return lax.dot_general(q_buf[h, pl.ds(qrow, QT), :], kk, (((1,), (1,)), ((), ())), preferred_element_type=F32)
-
-        def lane_sum(p):
-            s = p[:, :128]
-            for i in range(128, p.shape[1], 128):
-                s = s + p[:, i:i + 128]
-            return s
-
+            return lax.dot_general(kk, q_buf[h, pl.ds(qrow, QT), :], (((1,), (1,)), ((), ())), preferred_element_type=F32)
+
+        def weigh(d, row, count, p):
+            vv = v_buf[hp * 2 + d, pl.ds(row, count), :]
+            return lax.dot_general(vv, p.astype(BF16), (((0,), (0,)), ((), ())), preferred_element_type=F32)
+
+        s_all = [scores(d, qrow, QT) for d in range(2)]
         for d in range(2):
-            h = hp * 2 + d
-            s = scores(d, qrow, QT)
-            ri = lax.broadcasted_iota(jnp.int32, (QT, QT), 0)
-            ci = lax.broadcasted_iota(jnp.int32, (QT, QT), 1)
-            s = jnp.where(ci <= ri, s, NEG)
-            m = jnp.max(s, axis=-1, keepdims=True)
+            ki = lax.broadcasted_iota(jnp.int32, (QT, QT), 0)
+            qi = lax.broadcasted_iota(jnp.int32, (QT, QT), 1)
+            s = jnp.where(ki <= qi, s_all[d], NEG)
+            m = jnp.max(s, axis=0, keepdims=True)
             p = jnp.exp2((s - m) * scale)
-            m_ref[d] = jnp.broadcast_to(m, (QT, 128))
-            l_ref[d] = lane_sum(p)
-            acc[d] = jnp.dot(p.astype(BF16), v_buf[h, pl.ds(qrow, QT), :], preferred_element_type=F32)
+            m_ref[d] = m
+            l_ref[d] = jnp.sum(p, axis=0, keepdims=True)
+            acc[d] = weigh(d, qrow, QT, p)
 
         def update(row, count):
+            s_all = [scores(d, row, count) for d in range(2)]
             for d in range(2):
-                h = hp * 2 + d
-                s = scores(d, row, count)
-                m_old = m_ref[d][:, :1]
-                m = jnp.maximum(m_old, jnp.max(s, axis=-1, keepdims=True))
+                s = s_all[d]
+                m_old = m_ref[d]
+                m = jnp.maximum(m_old, jnp.max(s, axis=0, keepdims=True))
                 alpha = jnp.exp2((m_old - m) * scale)
                 p = jnp.exp2((s - m) * scale)
-                m_ref[d] = jnp.broadcast_to(m, (QT, 128))
-                l_ref[d] = l_ref[d] * alpha + lane_sum(p)
-                acc[d] = acc[d] * alpha + jnp.dot(p.astype(BF16), v_buf[h, pl.ds(row, count), :], preferred_element_type=F32)
+                m_ref[d] = m
+                l_ref[d] = l_ref[d] * alpha + jnp.sum(p, axis=0, keepdims=True)
+                acc[d] = acc[d] * alpha + weigh(d, row, count, p)
 
         def earlier_tile(kt, _):
             update(pl.multiple_of(first + kt * QT, QT), QT)
@@ -250,12 +247,13 @@
 
         for d in range(2):
             h = hp * 2 + d
-            denom = jnp.sum(l_ref[d], axis=-1, keepdims=True)
-            q_buf[h, pl.ds(qrow, QT), :] = (acc[d] / denom).astype(BF16)
+            out = acc[d] * (1.0 / l_ref[d])
+            q_buf[h, pl.ds(qrow, QT), :] = jnp.transpose(out).astype(BF16)
 
     early = rows // CHUNK // tiles
     n_early = 2
     n_units = 4 * tiles * 2
+    assert n_chunks == 8 and n_near == 3
 
     def far_step(i, _):
         is_unit = ((i >= early) & (i < early + n_early)) | (i >= n_chunks + n_early)
@@ -266,10 +264,11 @@
             cross_copy(k).wait_recv()
             diag_copy(k).start()
 
-            @pl.when((k >= n_near) & (k < n_chunks - 2))
-            def _():
-                cross_copy(k).wait_send()
-                cross_copy(k + 2).start()
+            @pl.when((k == 2) | (k == 5))
+            def _():
+                done = n_near + 2 * ((k - 2) // 3)
+                cross_copy(done).wait_send()
+                cross_copy(done + 2).start()
 
             @pl.when(k == n_chunks - 1)
             def _():
@@ -285,6 +284,11 @@
         def _():
             u = i - early * (1 - (i >= n_chunks + n_early).astype(jnp.int32)) - n_chunks * ((i >= n_chunks + n_early).astype(jnp.int32))
             attend(u)
+
+            @pl.when(u == 0)
+            def _():
+                cross_copy(n_near + 1).wait_send()
+                cross_copy(n_near + 3).start()
 
             @pl.when(u > n_early)
             def _():
@@ -330,9 +334,9 @@
             pltpu.VMEM((hl, seq, head_dim), BF16),
             pltpu.VMEM((PIECE, width), BF16),
             pltpu.VMEM((2, PIECE, head_dim // 2), F32),
-            pltpu.VMEM((2, QT, 128), F32),
-            pltpu.VMEM((2, QT, 128), F32),
-            pltpu.VMEM((2, QT, head_dim), F32),
+            pltpu.VMEM((2, 1, QT), F32),
+            pltpu.VMEM((2, 1, QT), F32),
+            pltpu.VMEM((2, head_dim, QT), F32),
             dma, dma((3 * hl,)), dma, dma,
             dma((n_chunks,)), dma((n_chunks,)), dma((n_chunks,)), dma((n_chunks,)),
             dma((4, tiles, hl)), dma((4, tiles, hl)), dma((tiles, hl)),

time: 400 us -> 394 us (0.985)
  Pallas kernels: 399 us -> 393 us
    pallas_call x1, Pallas kernels: 148 us -> 143 us  [attention(): pl.pallas_call(functools.partial(attention_kernel, rows, heads, head_dim)...]
where the time goes in v3:
time: 394 us
  Pallas kernels  393 us (100%)
    pallas_call x1, Pallas kernels, out_and_mlp(): pl.pallas_call(functools.partial(mlp_kernel, n_out, n_ff, bn), grid=(n_ou...  250 us
    pallas_call x1, Pallas kernels, attention(): pl.pallas_call(functools.partial(attention_kernel, rows, heads, head_dim)...  143 us

profile of v3, /device:TPU:0, one launch (start us, length us, event | category | flops | bytes accessed | tf_op | source)
XLA Modules:
  0.0 394.2 jit_solution(5344837748625394516)
XLA Ops:
  0.0 1.0 multiply_sine_fusion
  1.0 142.9 %gather_attention.1.o_ref = bf16[512,4096]{1,0:T(8,128)(2,1)} custom-call(bf16[512,4096]{1,0:T(8,128)(2,1)} %x_ref.1, f32[1,4096]{1,0:T(1,128)} %bitcast.4, bf16[4096,12288]{1,0:T(8,128)(2,1)} %w_hbm.1, f32[144,128]{1,0:T(8,128)} %get-tuple-element.6.cos_ref, f32[144,128]{1,0:T(8,128)} %get-tuple-element.5.sin_ref), custom_call_target="tpu_custom_call" | custom-call | tf_op jit(solution)/shard_map/gather_attention/pallas_call | solution.py:324
  143.9 250.3 %out_mlp.1 = bf16[512,4096]{1,0:T(8,128)(2,1)} custom-call(bf16[512,4096]{1,0:T(8,128)(2,1)} %gather_attention.1.o_ref, bf16[512,4096]{1,0:T(8,128)(2,1)} %x_ref.1, bf16[4096,4096]{1,0:T(8,128)(2,1)} %bitcast.3, f32[1,4096]{1,0:T(1,128)} %bitcast.5, bf16[4096,16384]{1,0:T(8,128)(2,1)} %wg_ref.1, bf16[4096,16384]{1,0:T(8,128)(2,1)} %wu_ref.1, ...), custom_call_target="tpu_custom_call" | custom-call | tf_op jit(solution)/shard_map/out_mlp/pallas_call | solution.py:406
  (4 shorter events, 0.0 us)
